TPU v7x, 32 devices: a whole 2x2x4 slice. The times are simulated.
32 devices in a mesh: shard: 4 (over y, x), rep: 8 (over z, core).
Axes of the slice: x: 2, y: 2, z: 4, core: 2. Of those that a mesh axis runs over, the one named last changes fastest.
Arguments:
- activations: bfloat16 [8, 512, 2048], P('rep', 'shard'), may hold values from -16 to 16
- segments: int32 [8, 512], P('rep'), may hold values from 0 to 3, never falling along the last dimension, each value on 1 to 256 neighbouring positions
- attn_gain: float32 [2048], replicated, may hold values from 0.25 to 1.75
- query_weight: bfloat16 [2048, 2048], P('shard'), may hold values from -0.125 to 0.125
- key_weight: bfloat16 [2048, 1024], P('shard'), may hold values from -0.125 to 0.125
- value_weight: bfloat16 [2048, 1024], P('shard'), may hold values from -0.125 to 0.125
- query_gain: float32 [128], replicated, may hold values from 0.5 to 5.5
- key_gain: float32 [128], replicated, may hold values from 0.5 to 5.5
- out_weight: bfloat16 [2048, 2048], P('shard'), may hold values from -0.75 to 0.75
- mlp_gain: float32 [2048], replicated, may hold values from 0.25 to 1.75
- gate_weight: bfloat16 [2048, 6144], P('shard'), may hold values from -0.125 to 0.125
- up_weight: bfloat16 [2048, 6144], P('shard'), may hold values from -0.125 to 0.125
- down_weight: bfloat16 [6144, 2048], P('shard'), may hold values from -0.078125 to 0.078125
- cotangent: bfloat16 [8, 512, 2048], P('rep', 'shard'), may hold values from -11.1 to 11.1
Outputs:
- output: bfloat16 [8, 512, 2048], P('rep', 'shard')
- grad_input: float32 [8, 512, 2048], P('rep', 'shard')
- grad_attn_gain: float32 [2048], replicated
- grad_query_weight: float32 [2048, 2048], P('shard')
- grad_key_weight: float32 [2048, 1024], P('shard')
- grad_value_weight: float32 [2048, 1024], P('shard')
- grad_query_gain: float32 [128], replicated
- grad_key_gain: float32 [128], replicated
- grad_out_weight: float32 [2048, 2048], P('shard')
- grad_mlp_gain: float32 [2048], replicated
- grad_gate_weight: float32 [2048, 6144], P('shard')
- grad_up_weight: float32 [2048, 6144], P('shard')
- grad_down_weight: float32 [6144, 2048], P('shard')
Inputs may be any that keep to these rules, and one draw needn't show every extreme that they name: `segments`: within each sequence the document numbers never fall; each document has 1 to 256 tokens, and one has exactly 256.
All inputs are finite; a program needn't handle non-finite values.
Results may differ from a plain program's by a relative error of at most 0.02.
The roundings to bfloat16 on the way count: a program that leaves them out, or rounds other values in their place, can miss the bound.
Values may be sent and summed in bfloat16 or wider, within the bound.
A program may use at most 384 MiB of HBM per device.

v0:
```python
from functools import partial
import math
import jax
import jax.numpy as jnp
from jax import lax
from jax.sharding import PartitionSpec as P

HQ = 16
HK = 8
HD = 128
FF = 6144
EPSILON = 1e-06
ROPE_BASE = 1000000.0
MASKED = -1e30


def dims_last(left_op, right_op):
    return lax.dot_general(
        left_op, right_op, (((1,), (1,)), ((), ())), preferred_element_type=jnp.float32
    )


def dims_first(left_op, right_op):
    return lax.dot_general(
        left_op, right_op, (((0,), (0,)), ((), ())), preferred_element_type=jnp.float32
    )


def positions(seg_ids):
    token_index = jnp.arange(seg_ids.shape[0], dtype=jnp.int32)
    before = jnp.concatenate([jnp.full((1,), -1, jnp.int32), seg_ids[:-1]])
    starts = lax.cummax(
        jnp.where(seg_ids != before, token_index, jnp.zeros_like(token_index)), axis=0
    )
    return (token_index - starts).astype(jnp.float32)


def rotary(pos_float):
    half_width = HD // 2
    inv_freq = 1.0 / ROPE_BASE ** (jnp.arange(half_width, dtype=jnp.float32) * (2.0 / HD))
    angles = pos_float[:, None] * inv_freq[None, :]
    return (jnp.cos(angles), jnp.sin(angles))


def rotate(values_in, cosine, sine_part):
    half_width = values_in.shape[-1] // 2
    first_half = values_in[..., :half_width]
    second_half = values_in[..., half_width:]
    cos_b = cosine[:, None, :]
    sin_b = sine_part[:, None, :]
    return jnp.concatenate(
        [first_half * cos_b - second_half * sin_b, second_half * cos_b + first_half * sin_b], -1
    )


def rotate_back(grads_in, cosine, sine_part):
    half_width = grads_in.shape[-1] // 2
    first_half = grads_in[..., :half_width]
    second_half = grads_in[..., half_width:]
    cos_b = cosine[:, None, :]
    sin_b = sine_part[:, None, :]
    return jnp.concatenate(
        [first_half * cos_b + second_half * sin_b, second_half * cos_b - first_half * sin_b], -1
    )


def norm_back(grad_normed, values_in, rstat, gain_vec):
    scaled = values_in * rstat
    lead_axes = tuple(range(grad_normed.ndim - 1))
    grad_gain = jnp.sum(grad_normed * scaled, axis=lead_axes)
    weighted = grad_normed * gain_vec
    grad_values = rstat * (weighted - scaled * jnp.mean(weighted * scaled, -1, keepdims=True))
    return (grad_values, grad_gain)


def head_scores(query_group, key_block, visible, score_scale):
    scores = (
        jnp.einsum("qgd,kd->gqk", query_group, key_block, preferred_element_type=jnp.float32)
        * score_scale
    )
    return jnp.where(visible[None], scores, MASKED)


def attend(head_item, visible, score_scale):
    query_group, key_block, value_block = head_item
    scores = head_scores(query_group, key_block, visible, score_scale)
    row_max = jnp.max(scores, -1, keepdims=True)
    exp_scores = jnp.exp(scores - row_max)
    row_total = jnp.sum(exp_scores, -1, keepdims=True)
    softmax_out = (exp_scores / row_total).astype(jnp.bfloat16)
    head_out = jnp.einsum(
        "gqk,kd->qgd", softmax_out, value_block, preferred_element_type=jnp.float32
    )
    return (head_out, row_max + jnp.log(row_total))


def attend_back(head_item, visible, score_scale):
    query_group, key_block, value_block, grad_head, log_total = head_item
    scores = head_scores(query_group, key_block, visible, score_scale)
    softmax_out = jnp.exp(scores - log_total)
    grad_soft = jnp.einsum(
        "qgd,kd->gqk", grad_head, value_block, preferred_element_type=jnp.float32
    )
    row_delta = jnp.sum(softmax_out * grad_soft, -1, keepdims=True)
    grad_scores = (softmax_out * (grad_soft - row_delta)).astype(jnp.bfloat16)
    grad_group = (
        jnp.einsum("gqk,kd->qgd", grad_scores, key_block, preferred_element_type=jnp.float32)
        * score_scale
    )
    grad_key = (
        jnp.einsum("gqk,qgd->kd", grad_scores, query_group, preferred_element_type=jnp.float32)
        * score_scale
    )
    grad_value = jnp.einsum(
        "gqk,qgd->kd",
        softmax_out.astype(jnp.bfloat16),
        grad_head,
        preferred_element_type=jnp.float32,
    )
    return (grad_group, grad_key, grad_value)


def per_device(
    activations,
    segments,
    attn_gain,
    query_weight,
    key_weight,
    value_weight,
    query_gain,
    key_gain,
    out_weight,
    mlp_gain,
    gate_weight,
    up_weight,
    down_weight,
    cotangent,
):
    tok_rows = activations.shape[1]
    length = segments.shape[1]
    groups = HQ // HK
    score_scale = 1.0 / math.sqrt(HD)
    offset = lax.axis_index("shard") * tok_rows
    seg_ids = segments[0]
    pos_float = lax.dynamic_slice_in_dim(positions(seg_ids), offset, tok_rows)
    cosine, sine_part = rotary(pos_float)
    key_index = jnp.arange(length, dtype=jnp.int32)
    query_rows = offset + jnp.arange(tok_rows, dtype=jnp.int32)
    seg_rows = lax.dynamic_slice_in_dim(seg_ids, offset, tok_rows)
    visible = (key_index[None, :] <= query_rows[:, None]) & (seg_ids[None, :] == seg_rows[:, None])
    inputs = activations[0].astype(jnp.float32)
    rstat_attn = lax.rsqrt(jnp.mean(inputs * inputs, -1, keepdims=True) + EPSILON)
    normed = (inputs * rstat_attn * attn_gain).astype(jnp.bfloat16)
    full_query, full_key, full_value, full_out = (
        lax.all_gather(query_weight, "shard", axis=0, tiled=True),
        lax.all_gather(key_weight, "shard", axis=0, tiled=True),
        lax.all_gather(value_weight, "shard", axis=0, tiled=True),
        lax.all_gather(out_weight, "shard", axis=0, tiled=True),
    )
    queries = jnp.dot(normed, full_query, preferred_element_type=jnp.float32).reshape(
        tok_rows, HQ, HD
    )
    keys_raw = jnp.dot(normed, full_key, preferred_element_type=jnp.float32).reshape(
        tok_rows, HK, HD
    )
    values_low = jnp.dot(normed, full_value, preferred_element_type=jnp.float32).astype(
        jnp.bfloat16
    )
    query_rstat = lax.rsqrt(jnp.mean(queries * queries, -1, keepdims=True) + EPSILON)
    key_rstat = lax.rsqrt(jnp.mean(keys_raw * keys_raw, -1, keepdims=True) + EPSILON)
    query_rot = rotate(queries * query_rstat * query_gain, cosine, sine_part).astype(jnp.bfloat16)
    key_rot = rotate(keys_raw * key_rstat * key_gain, cosine, sine_part).astype(jnp.bfloat16)
    key_heads = jnp.transpose(key_rot, (1, 0, 2))
    value_heads = jnp.transpose(values_low.reshape(tok_rows, HK, HD), (1, 0, 2))
    all_keys, all_values = (
        lax.all_gather(key_heads, "shard", axis=1, tiled=True),
        lax.all_gather(value_heads, "shard", axis=1, tiled=True),
    )
    query_heads = jnp.transpose(query_rot.reshape(tok_rows, HK, groups, HD), (1, 0, 2, 3))
    attn_heads, log_totals = lax.map(
        partial(attend, visible=visible, score_scale=score_scale),
        (query_heads, all_keys, all_values),
    )
    attn_out = (
        jnp.transpose(attn_heads, (1, 0, 2, 3)).reshape(tok_rows, HQ * HD).astype(jnp.bfloat16)
    )
    hidden = inputs + jnp.dot(attn_out, full_out, preferred_element_type=jnp.float32)
    rstat_mlp = lax.rsqrt(jnp.mean(hidden * hidden, -1, keepdims=True) + EPSILON)
    normed_mlp = (hidden * rstat_mlp * mlp_gain).astype(jnp.bfloat16)
    full_gate, full_up, full_down = (
        lax.all_gather(gate_weight, "shard", axis=0, tiled=True),
        lax.all_gather(up_weight, "shard", axis=0, tiled=True),
        lax.all_gather(down_weight, "shard", axis=0, tiled=True),
    )
    gate_pre = jnp.dot(normed_mlp, full_gate, preferred_element_type=jnp.float32)
    up_pre = jnp.dot(normed_mlp, full_up, preferred_element_type=jnp.float32)
    sigmoid_gate = jax.nn.sigmoid(gate_pre)
    activated = (gate_pre * sigmoid_gate * up_pre).astype(jnp.bfloat16)
    result = hidden + jnp.dot(activated, full_down, preferred_element_type=jnp.float32)
    output = result.astype(jnp.bfloat16)[None]
    grad_out = cotangent[0]
    back_gate, back_up, back_down = (
        lax.all_gather(gate_weight, "shard", axis=0, tiled=True),
        lax.all_gather(up_weight, "shard", axis=0, tiled=True),
        lax.all_gather(down_weight, "shard", axis=0, tiled=True),
    )
    grad_act = dims_last(grad_out, back_down)
    grad_gate = (grad_act * up_pre * sigmoid_gate * (1.0 + gate_pre * (1.0 - sigmoid_gate))).astype(
        jnp.bfloat16
    )
    grad_up = (grad_act * gate_pre * sigmoid_gate).astype(jnp.bfloat16)
    grad_normed_mlp = dims_last(grad_gate, back_gate) + dims_last(grad_up, back_up)
    grad_hidden_part, grad_mlp_gain = norm_back(grad_normed_mlp, hidden, rstat_mlp, mlp_gain)
    grad_hidden = grad_out.astype(jnp.float32) + grad_hidden_part
    grad_branch = grad_hidden.astype(jnp.bfloat16)
    back_query, back_key, back_value, back_out = (
        lax.all_gather(query_weight, "shard", axis=0, tiled=True),
        lax.all_gather(key_weight, "shard", axis=0, tiled=True),
        lax.all_gather(value_weight, "shard", axis=0, tiled=True),
        lax.all_gather(out_weight, "shard", axis=0, tiled=True),
    )
    grad_attn = dims_last(grad_branch, back_out).astype(jnp.bfloat16)
    grad_heads = jnp.transpose(grad_attn.reshape(tok_rows, HK, groups, HD), (1, 0, 2, 3))
    grad_query_heads, grad_keys_all, grad_values_all = lax.map(
        partial(attend_back, visible=visible, score_scale=score_scale),
        (query_heads, all_keys, all_values, grad_heads, log_totals),
    )
    own_keys, own_values = (
        lax.psum_scatter(
            grad_keys_all.astype(jnp.bfloat16), "shard", scatter_dimension=1, tiled=True
        ).astype(jnp.float32),
        lax.psum_scatter(
            grad_values_all.astype(jnp.bfloat16), "shard", scatter_dimension=1, tiled=True
        ).astype(jnp.float32),
    )
    grad_query_rot = jnp.transpose(grad_query_heads, (1, 0, 2, 3)).reshape(tok_rows, HQ, HD)
    grad_key_rot = jnp.transpose(own_keys, (1, 0, 2))
    grad_value = (
        jnp.transpose(own_values, (1, 0, 2)).reshape(tok_rows, HK * HD).astype(jnp.bfloat16)
    )
    grad_query_norm, grad_query_gain = norm_back(
        rotate_back(grad_query_rot, cosine, sine_part), queries, query_rstat, query_gain
    )
    grad_key_norm, grad_key_gain = norm_back(
        rotate_back(grad_key_rot, cosine, sine_part), keys_raw, key_rstat, key_gain
    )
    grad_query = grad_query_norm.reshape(tok_rows, HQ * HD).astype(jnp.bfloat16)
    grad_key = grad_key_norm.reshape(tok_rows, HK * HD).astype(jnp.bfloat16)
    grad_normed = (
        dims_last(grad_query, back_query)
        + dims_last(grad_key, back_key)
        + dims_last(grad_value, back_value)
    )
    grad_input_part, grad_attn_gain = norm_back(grad_normed, inputs, rstat_attn, attn_gain)
    grad_input = (grad_hidden + grad_input_part)[None]
    grad_attn_gain, grad_query_gain, grad_key_gain, grad_mlp_gain = lax.psum(
        (grad_attn_gain, grad_query_gain, grad_key_gain, grad_mlp_gain), ("shard", "rep")
    )
    grad_qkv = jnp.concatenate([grad_query, grad_key, grad_value], 1)
    grad_mlp = jnp.concatenate([grad_gate, grad_up], 1)
    cols_attn, cols_mlp, cols_heads, cols_act = (
        lax.all_to_all(normed, "shard", split_axis=1, concat_axis=0, tiled=True),
        lax.all_to_all(normed_mlp, "shard", split_axis=1, concat_axis=0, tiled=True),
        lax.all_to_all(attn_out, "shard", split_axis=1, concat_axis=0, tiled=True),
        lax.all_to_all(activated, "shard", split_axis=1, concat_axis=0, tiled=True),
    )
    piece_qkv = lax.all_gather(grad_qkv, "shard", axis=0, tiled=True)
    piece_mlp = lax.all_gather(grad_mlp, "shard", axis=0, tiled=True)
    piece_branch = lax.all_gather(grad_branch, "shard", axis=0, tiled=True)
    piece_out = lax.all_gather(grad_out, "shard", axis=0, tiled=True)
    added_in = jnp.concatenate(
        [dims_first(cols_attn, piece_qkv), dims_first(cols_mlp, piece_mlp)], 1
    )
    part_out = dims_first(cols_heads, piece_branch)
    part_down = dims_first(cols_act, piece_out)
    owned_in, owned_out, owned_down = (
        lax.psum(added_in.astype(jnp.bfloat16), "rep").astype(jnp.float32),
        lax.psum(part_out.astype(jnp.bfloat16), "rep").astype(jnp.float32),
        lax.psum(part_down.astype(jnp.bfloat16), "rep").astype(jnp.float32),
    )
    width_query = HQ * HD
    width_kv = HK * HD
    edge_key = width_query + width_kv
    edge_value = edge_key + width_kv
    edge_gate = edge_value + FF
    grad_query_weight = owned_in[:, :width_query]
    grad_key_weight = owned_in[:, width_query:edge_key]
    grad_value_weight = owned_in[:, edge_key:edge_value]
    grad_gate_weight = owned_in[:, edge_value:edge_gate]
    grad_up_weight = owned_in[:, edge_gate:]
    return (
        output,
        grad_input,
        grad_attn_gain,
        grad_query_weight,
        grad_key_weight,
        grad_value_weight,
        grad_query_gain,
        grad_key_gain,
        owned_out,
        grad_mlp_gain,
        grad_gate_weight,
        grad_up_weight,
        owned_down,
    )


def solution(mesh):
    placed = (
        P("rep", "shard", None),
        P("rep", None),
        P(),
        P("shard", None),
        P("shard", None),
        P("shard", None),
        P(),
        P(),
        P("shard", None),
        P(),
        P("shard", None),
        P("shard", None),
        P("shard", None),
        P("rep", "shard", None),
    )
    return jax.shard_map(
        per_device,
        mesh=mesh,
        in_specs=placed,
        out_specs=(
            P("rep", "shard", None),
            P("rep", "shard", None),
            P(),
            P("shard", None),
            P("shard", None),
            P("shard", None),
            P(),
            P(),
            P("shard", None),
            P(),
            P("shard", None),
            P("shard", None),
            P("shard", None),
        ),
        check_vma=False,
    )
```

profile of v0, /device:TPU:0, one launch (start us, length us, event | category | flops | bytes accessed | tf_op | source)
XLA Modules:
  0.0 2083.6 jit_solution(7904533563809124515)
XLA Ops:
  11.7 53.4 %all-gather.19.cloned.1.call-done = bf16[2048,1024]{1,0:T(8,128)(2,1)} async-done(((bf16[512,1024]{1,0:T(8,128)(2,1)}), bf16[2048,1024]{1,0:T(8,128)(2,1)}) %all-gather.19.cloned.1.call-update) | async-done | bytes 4194320 | tf_op jit(solution)/shard_map/all_gather | solution.py:156
  65.2 6.5 copy.79
  71.7 3.7 multiply_reduce_fusion.9
  77.7 41.9 %all-gather.15.cloned.1.call-done = bf16[2048,1024]{1,0:T(8,128)(2,1)} async-done(((bf16[512,1024]{1,0:T(8,128)(2,1)}), bf16[2048,1024]{1,0:T(8,128)(2,1)}) %all-gather.15.cloned.1.call-update) | async-done | bytes 4194320 | tf_op jit(solution)/shard_map/all_gather | solution.py:157
  119.6 3.0 fusion.53
  128.3 20.1 all-gather.21.cloned.1.call-done
  150.0 87.6 %all-gather.23.cloned.1.call-done = bf16[2048,2048]{1,0:T(8,128)(2,1)} async-done(((bf16[512,2048]{1,0:T(8,128)(2,1)}), bf16[2048,2048]{1,0:T(8,128)(2,1)}) %all-gather.23.cloned.1.call-update) | async-done | bytes 8388624 | tf_op jit(solution)/shard_map/all_gather | solution.py:155
  237.6 12.2 copy.80
  249.9 5.8 multiply_reduce_fusion.6
  259.7 6.7 all-gather.17.cloned.1.call-done
  266.4 28.7 %while.30 = (s32[]{:T(128)}, bf16[8,128,2,128]{1,3,2,0:T(8,128)(2,1)}, f32[8,2,128,1]{2,1,3,0:T(2,128)}, bf16[8,512,128]{2,1,0:T(8,128)(2,1)}, bf16[8,512,128]{2...) while((s32[]{:T(128)}, ...), condition=%wide.region_8.9_spmd.clone.clone, body=%wide.region_5.8_spmd.clone.sunk.clone | while | flops 68353792 | bytes 2176605 | solution.py:180
  271.7 1.8 fusion.163
  275.3 1.8 fusion.163
  278.9 1.8 fusion.163
  295.1 60.5 %all-gather.25.cloned.1.call-done = bf16[2048,2048]{1,0:T(8,128)(2,1)} async-done(((bf16[512,2048]{1,0:T(8,128)(2,1)}), bf16[2048,2048]{1,0:T(8,128)(2,1)}) %all-gather.25.cloned.1.call-update) | async-done | bytes 8388624 | tf_op jit(solution)/shard_map/all_gather | solution.py:158
  355.6 4.9 multiply_reduce_fusion.5
  360.8 224.3 %all-gather.27.cloned.1.call-done = bf16[2048,6144]{1,0:T(8,128)(2,1)} async-done(((bf16[512,6144]{1,0:T(8,128)(2,1)}), bf16[2048,6144]{1,0:T(8,128)(2,1)}) %all-gather.27.cloned.1.call-update) | async-done | bytes 25165840 | tf_op jit(solution)/shard_map/all_gather | solution.py:191
  585.1 13.7 fusion.86
  598.8 215.8 %all-gather.29.cloned.1.call-done = bf16[2048,6144]{1,0:T(8,128)(2,1)} async-done(((bf16[512,6144]{1,0:T(8,128)(2,1)}), bf16[2048,6144]{1,0:T(8,128)(2,1)}) %all-gather.29.cloned.1.call-update) | async-done | bytes 25165840 | tf_op jit(solution)/shard_map/all_gather | solution.py:192
  814.6 13.7 fusion.87
  828.3 215.8 %all-gather.31.cloned.1.call-done = bf16[6144,2048]{1,0:T(8,128)(2,1)} async-done(((bf16[1536,2048]{1,0:T(8,128)(2,1)}), bf16[6144,2048]{1,0:T(8,128)(2,1)}) %all-gather.31.cloned.1.call-update) | async-done | bytes 25165840 | tf_op jit(solution)/shard_map/all_gather | solution.py:193
  1044.1 16.8 multiply_convert_fusion.1
  1060.9 14.5 fusion.88
  1075.4 15.3 multiply_reduce_fusion.1
  1090.7 2.4 fusion.82
  1093.1 6.4 convolution_convert_fusion.4
  1100.7 2.0 copy.140
  1102.7 86.9 %while.31 = (s32[]{:T(128)}, f32[8,128,2,128]{1,3,2,0:T(8,128)}, bf16[8,512,128]{1,2,0:T(8,128)(2,1)}, bf16[8,512,128]{1,2,0:T(8,128)(2,1)}, bf16[8,512,128]{2,1...) while((s32[]{:T(128)}, f32[8,128,2,128]{1,3,2,0:T(8,128)}, ...), condition=%wide.region_13.14_spmd.clone.clone, body=%wide.region_11.13_spmd.clone.sunk.clone | while | flops 169312000 | bytes 5780601 | solution.py:224
  1189.6 2.4 copy.97
  1192.0 2.5 copy.138
  1194.6 2.4 copy.99
  1197.0 2.5 copy.137
  1204.2 18.4 reduce-scatter.7.cloned.1.call-done
  1223.8 30.2 %reduce-scatter.9.cloned.1.call-done = bf16[128,1024]{1,0:T(8,128)(2,1)} async-done(((bf16[512,1024]{1,0:T(8,128)(2,1)}), bf16[128,1024]{1,0:T(8,128)(2,1)}) %reduce-scatter.9.cloned.1.call-update) | async-done | bytes 262160
  1256.8 3.8 pad_maximum_fusion.1
  1260.7 4.2 all-to-all-start.2
  1264.9 2.7 copy.136
  1267.6 9.6 all-to-all-done.2
  1277.3 4.4 all-to-all-start.3
  1283.4 2.4 fusion.56
  1286.6 2.0 copy.91
  1288.6 23.6 %all-to-all-done.3 = bf16[128,4,1536]{2,0,1:T(8,128)(2,1)} async-done(((bf16[128,4,1536]{2,0,1:T(8,128)(2,1)}), bf16[128,4,1536]{2,0,1:T(8,128)(2,1)}, u32[]{:S(2)}, u32[]{:S(2)}) %all-to-all-start.3) | async-done | bytes 1572896 | tf_op jit(solution)/shard_map/all_to_all | solution.py:265
  1312.3 3.5 all-to-all-start
  1315.8 8.2 convolution_convert_fusion.1
  1324.0 25.4 %all-gather.37.cloned.1.call-done = bf16[512,2048]{1,0:T(8,128)(2,1)} async-done(((bf16[128,2048]{1,0:T(8,128)(2,1)}), bf16[512,2048]{1,0:T(8,128)(2,1)}) %all-gather.37.cloned.1.call-update) | async-done | bytes 2097168 | tf_op jit(solution)/shard_map/all_gather | solution.py:269
  1349.5 4.4 convolution_convert_fusion.3
  1354.6 3.5 all-to-all-start.1
  1358.2 49.5 %all-gather.33.cloned.1.call-done = bf16[512,4096]{0,1:T(8,128)(2,1)} async-done(((bf16[128,4096]{0,1:T(8,128)(2,1)}), bf16[512,4096]{0,1:T(8,128)(2,1)}) %all-gather.33.cloned.1.call-update) | async-done | bytes 4194320 | tf_op jit(solution)/shard_map/all_gather | solution.py:267
  1407.7 6.8 convolution_convert_fusion.2
  1414.5 117.9 %all-gather.35.cloned.1.call-done = bf16[512,12288]{1,0:T(8,128)(2,1)} async-done(((bf16[128,12288]{1,0:T(8,128)(2,1)}), bf16[512,12288]{1,0:T(8,128)(2,1)}) %all-gather.35.cloned.1.call-update) | async-done | bytes 12582928 | tf_op jit(solution)/shard_map/all_gather | solution.py:268
  1532.4 11.7 convolution_convert_fusion
  1544.1 9.0 pad_maximum_fusion
  1553.2 6.4 fusion.89
  1559.6 11.3 fusion.51
  1573.2 2.7 fusion.67
  1575.8 41.9 %all-reduce = (f32[2048]{0:T(1024)}, f32[128]{0:T(128)}, f32[128]{0:T(128)}, f32[2048]{0:T(1024)}) all-reduce(f32[2048]{0:T(1024)S(1)} %get-tuple-element.250, f32[128]{0:T(128)S(1)} %get-tuple-element.246, f32[128]{0:T(128)S(1)} %get-tuple-element.252, f32[2048]{0:T(1024)S(1)} %copy-done.29), channel_id=1, replica_groups=mesh['shard'=4,'rep'=8] {'shard','rep'}, use_global_device_ids=true, to_apply=%region_20.21 | all-reduce | flops 4352 | bytes 34816 | tf_op jit(solution)/shard_map/psum | solution.py:256
  1617.8 2.8 fusion.66
  1620.5 424.3 %all-reduce.4.cloned.1.call-done = (bf16[512,16384]{1,0:T(8,128)(2,1)}, bf16[512,2048]{1,0:T(8,128)(2,1)}, bf16[1536,2048]{1,0:T(8,128)(2,1)}) async-done(((bf16[512,16384]{1,0:T(8,128)(2,1)}, bf16[512,2048]{1,0:T(8,128)(2,1)}, bf16[1536,2048]{1,0:T(8,128)(2,1)}), (bf16[512,16384]{1,0:T(8,128)(2,1)}, bf16[512,2048]{1,0:T(8,128)(2,1)}, bf16[1536,2048]{1,0:T(8,128)(2,1)})) %all-reduce.4.cloned.1.call-update) | async-done | bytes 25165840 | tf_op jit(solution)/shard_map/psum | solution.py:277
  2044.9 15.6 fusion.84
  2060.4 2.4 copy-done
  2062.9 2.6 fusion.85
  2065.5 2.5 slice.77
  2068.0 6.3 convert_element_type.162
  2074.3 2.5 convert_element_type.160
  (289 shorter events, 143.3 us)
Async XLA Ops:
  7.2 58.0 %all-gather.19.cloned.1.call-start = ((), (), s32[]{:S(2)}) async-start(), calls=%async_computation.8 | async-start | bytes 5242880 | tf_op jit(solution)/shard_map/all_gather | solution.py:156
  7.9 111.7 %all-gather.15.cloned.1.call-start = ((), (), s32[]{:S(2)}) async-start(), calls=%async_computation.6 | async-start | bytes 5242880 | tf_op jit(solution)/shard_map/all_gather | solution.py:157
  8.7 139.7 %all-gather.21.cloned.1.call-start = ((), (), s32[]{:S(2)}) async-start(), calls=%async_computation.9 | async-start | bytes 1310720 | tf_op jit(solution)/shard_map/all_gather | solution.py:176
  11.5 238.4 %copy-start.30 = (f32[128]{0:T(128)}, f32[128]{0:T(128)S(1)}, u32[]{:S(2)}) copy-start(f32[128]{0:T(128)S(1)} %add_rsqrt_fusion.3) | copy-start | bytes 1540
  11.7 244.3 %copy-start.18 = (f32[128,64]{0,1:T(8,128)}, f32[128,64]{0,1:T(8,128)S(1)}, u32[]{:S(2)}) copy-start(f32[128,64]{0,1:T(8,128)S(1)} %get-tuple-element.322) | copy-start | bytes 98308
  11.7 244.3 %copy-start.20 = (f32[128,64]{0,1:T(8,128)}, f32[128,64]{0,1:T(8,128)S(1)}, u32[]{:S(2)}) copy-start(f32[128,64]{0,1:T(8,128)S(1)} %get-tuple-element.323) | copy-start | bytes 98308
  65.2 6.5 copy-start.1
  65.2 6.5 copy-start.24
  71.6 4.5 copy-start.34
  75.4 0.8 copy-start.8
  77.1 160.5 %all-gather.23.cloned.1.call-start = ((), (), s32[]{:S(2)}) async-start(), calls=%async_computation.10 | async-start | bytes 10485760 | tf_op jit(solution)/shard_map/all_gather | solution.py:155
  77.7 188.7 %all-gather.17.cloned.1.call-start = ((), (), s32[]{:S(2)}) async-start(), calls=%async_computation.7 | async-start | bytes 1310720 | tf_op jit(solution)/shard_map/all_gather | solution.py:177
  123.3 232.3 %all-gather.25.cloned.1.call-start = ((), (), s32[]{:S(2)}) async-start(), calls=%async_computation.11 | async-start | bytes 10485760 | tf_op jit(solution)/shard_map/all_gather | solution.py:158
  123.9 461.2 %all-gather.27.cloned.1.call-start = ((), (), s32[]{:S(2)}) async-start(), calls=%async_computation.12 | async-start | bytes 31457280 | tf_op jit(solution)/shard_map/all_gather | solution.py:191
  124.7 689.9 %all-gather.29.cloned.1.call-start = ((), (), s32[]{:S(2)}) async-start(), calls=%async_computation.13 | async-start | bytes 31457280 | tf_op jit(solution)/shard_map/all_gather | solution.py:192
  125.4 0.8 copy-start.23
  125.4 918.6 %all-gather.31.cloned.1.call-start = ((), (), s32[]{:S(2)}) async-start(), calls=%async_computation.14 | async-start | bytes 31457280 | tf_op jit(solution)/shard_map/all_gather | solution.py:193
  126.2 1096.4 %reduce-scatter.7.cloned.1.call-start = ((), (), s32[]{:S(2)}) async-start(), calls=%async_computation.19 | async-start | bytes 1310720
  249.9 5.9 copy-start.36
  255.7 10.7 copy-start.27
  295.1 60.5 %copy-start.7 = (bf16[8,512,128]{2,1,0:T(8,128)(2,1)}, bf16[8,512,128]{2,1,0:T(8,128)(2,1)S(1)}, u32[]{:S(2)}) copy-start(bf16[8,512,128]{2,1,0:T(8,128)(2,1)S(1)} %get-tuple-element.616) | copy-start | bytes 3145732
  295.1 60.5 %copy-start.14 = (bf16[8,128,2,128]{3,1,2,0:T(8,128)(2,1)}, bf16[8,128,2,128]{3,1,2,0:T(8,128)(2,1)S(1)}, u32[]{:S(2)}) copy-start(bf16[8,128,2,128]{3,1,2,0:T(8,128)(2,1)S(1)} %get-tuple-element.632) | copy-start | bytes 1572868
  355.6 5.0 copy-start.25
  360.6 730.1 %copy-start.32 = (f32[128]{0:T(128)}, f32[128]{0:T(128)S(1)}, u32[]{:S(2)}) copy-start(f32[128]{0:T(128)S(1)} %add_rsqrt_fusion.2) | copy-start | bytes 1540
  360.8 453.8 %copy-start.4 = (bf16[128,2048]{1,0:T(8,128)(2,1)}, bf16[128,2048]{1,0:T(8,128)(2,1)S(1)}, u32[]{:S(2)}) copy-start(bf16[128,2048]{1,0:T(8,128)(2,1)S(1)} %multiply_convert_fusion.5) | copy-start | bytes 1572868
  1075.4 15.3 copy-start.11
  1090.7 8.8 copy-start.38
  1194.5 6.8 copy-start.19
  1194.5 6.8 copy-start.21
  1194.5 59.5 %reduce-scatter.9.cloned.1.call-start = ((), (), s32[]{:S(2)}) async-start(), calls=%async_computation.20 | async-start | bytes 1310720
  1194.5 8.1 copy-start.28
  1194.5 8.1 copy-start.37
  1199.5 116.3 %all-gather.39.cloned.1.call-start = ((), (), s32[]{:S(2)}) async-start(), calls=%async_computation.18 | async-start | bytes 2621440 | tf_op jit(solution)/shard_map/all_gather | solution.py:270
  1200.1 149.4 %all-gather.37.cloned.1.call-start = ((), (), s32[]{:S(2)}) async-start(), calls=%async_computation.17 | async-start | bytes 2621440 | tf_op jit(solution)/shard_map/all_gather | solution.py:269
  1200.8 206.9 %all-gather.33.cloned.1.call-start = ((), (), s32[]{:S(2)}) async-start(), calls=%async_computation.15 | async-start | bytes 5242880 | tf_op jit(solution)/shard_map/all_gather | solution.py:267
  1202.7 52.7 %copy-start.9 = (f32[128,8,128]{0,2,1:T(8,128)S(1)}, f32[128,8,128]{0,2,1:T(8,128)}, u32[]{:S(2)}) copy-start(f32[128,8,128]{0,2,1:T(8,128)} %copy-done.8) | copy-start | bytes 1572868
  1202.7 52.7 %copy-start.35 = (f32[128]{0:T(128)S(1)}, f32[128]{0:T(128)}, u32[]{:S(2)}) copy-start(f32[128]{0:T(128)} %param.25) | copy-start | bytes 1540
  1204.2 51.5 %copy-start.13 = (bf16[128,16,128]{0,2,1:T(8,128)(2,1)S(1)}, bf16[128,16,128]{0,2,1:T(8,128)(2,1)}, u32[]{:S(2)}) copy-start(bf16[128,16,128]{0,2,1:T(8,128)(2,1)} %multiply_convert_fusion.4) | copy-start | bytes 1572868
  1255.2 5.4 copy-start.15
  1256.8 275.6 %all-gather.35.cloned.1.call-start = ((), (), s32[]{:S(2)}) async-start(), calls=%async_computation.16 | async-start | bytes 15728640 | tf_op jit(solution)/shard_map/all_gather | solution.py:268
  1260.7 16.6 all-to-all-start.2
  1264.9 18.5 copy-start.31
  1264.9 20.9 %copy-start.5 = (bf16[128,2048]{1,0:T(8,128)(2,1)S(1)}, bf16[128,2048]{1,0:T(8,128)(2,1)}, u32[]{:S(2)}) copy-start(bf16[128,2048]{1,0:T(8,128)(2,1)} %copy-done.4) | copy-start | bytes 1572868
  1277.3 35.0 %all-to-all-start.3 = ((bf16[128,4,1536]{2,0,1:T(8,128)(2,1)}), bf16[128,4,1536]{2,0,1:T(8,128)(2,1)}, u32[]{:S(2)}, u32[]{:S(2)}) async-start(bf16[128,4,1536]{2,0,1:T(8,128)(2,1)} %bitcast.331), calls=%async_computation.3 | async-start | bytes 3145728 | tf_op jit(solution)/shard_map/all_to_all | solution.py:265
  1312.3 41.6 %all-to-all-start = ((bf16[128,4,512]{2,0,1:T(8,128)(2,1)}), bf16[128,4,512]{2,0,1:T(8,128)(2,1)S(1)}, u32[]{:S(2)}, u32[]{:S(2)}) async-start(bf16[128,4,512]{2,0,1:T(8,128)(2,1)} %fusion.56), calls=%async_computation | async-start | bytes 1048576 | tf_op jit(solution)/shard_map/all_to_all | solution.py:262
  1353.8 0.8 copy-start.22
  1354.6 59.8 %all-to-all-start.1 = ((bf16[128,4,512]{2,0,1:T(8,128)(2,1)}), bf16[128,4,512]{2,0,1:T(8,128)(2,1)S(1)}, u32[]{:S(2)}, u32[]{:S(2)}) async-start(bf16[128,4,512]{2,0,1:T(8,128)(2,1)} %bitcast.345), calls=%async_computation.1 | async-start | bytes 1048576 | tf_op jit(solution)/shard_map/all_to_all | solution.py:263
  1358.1 686.8 %all-reduce.4.cloned.1.call-start = ((), (), s32[]{:S(2)}) async-start(), calls=%async_computation.21 | async-start | bytes 50331648 | tf_op jit(solution)/shard_map/psum | solution.py:277
  1553.1 6.4 copy-start.10
  1559.6 11.3 copy-start.3
  1570.9 2.2 copy-start.2
  1570.9 2.3 copy-start.16
  1573.1 2.7 copy-start.29
  1573.1 44.6 %copy-start.6 = (f32[128,2048]{1,0:T(8,128)S(1)}, f32[128,2048]{1,0:T(8,128)}, u32[]{:S(2)}) copy-start(f32[128,2048]{1,0:T(8,128)} %get-tuple-element.330) | copy-start | bytes 3145732
  1573.1 44.6 %copy-start.12 = (bf16[1,128,2048]{2,1,0:T(8,128)(2,1)S(1)}, bf16[1,128,2048]{2,1,0:T(8,128)(2,1)}, u32[]{:S(2)}) copy-start(bf16[1,128,2048]{2,1,0:T(8,128)(2,1)} %param.31) | copy-start | bytes 1572868
  1573.1 44.6 %copy-start.26 = (f32[2048]{0:T(1024)S(1)}, f32[2048]{0:T(1024)}, u32[]{:S(2)}) copy-start(f32[2048]{0:T(1024)} %param.27) | copy-start | bytes 24580
  1573.1 44.6 %copy-start.33 = (f32[128]{0:T(128)S(1)}, f32[128]{0:T(128)}, u32[]{:S(2)}) copy-start(f32[128]{0:T(128)} %copy-done.32) | copy-start | bytes 1540
  1573.1 44.6 %copy-start.39 = (f32[128]{0:T(128)S(1)}, f32[128]{0:T(128)}, u32[]{:S(2)}) copy-start(f32[128]{0:T(128)} %copy-done.38) | copy-start | bytes 1540
  2044.9 18.0 copy-start
  2062.9 5.1 slice-start
  2065.5 2.6 slice-start.1
  2068.0 6.3 copy-start.17
Sparse Core Ops, SparseCore 0:
  9.8 55.2 all-gather.18
  67.0 52.5 all-gather.14
  122.0 26.3 all-gather.20
  150.1 87.4 all-gather.22
  239.9 26.4 all-gather.16
  268.1 87.4 all-gather.24
  357.5 227.5 all-gather.26
  587.0 227.5 all-gather.28
  816.4 227.5 all-gather.30
  1194.6 27.9 reduce-scatter.6
  1226.0 27.9 reduce-scatter.8
  1255.7 56.7 all-gather.38
  1314.3 35.1 all-gather.36
  1351.7 55.9 all-gather.32
  1410.0 122.3 all-gather.34
  1553.3 491.5 all-reduce.3
where the time goes:
time: 2090 us; the launch traced here: 2080 us
  waiting for transfers between devices  1630 us (78%)
  matrix products  228 us (11%)
  local copies, waits for them, and re-layouts  91.2 us (4%)
  other arithmetic  59.5 us (3%)
  blocking collectives  41.9 us (2%)
    psum x1, waiting for transfers between devices, per_device(): lax.psum(added_in.astype(jnp.bfloat16), 'rep').astype(jnp.float32)  424 us
    all_gather x1, waiting for transfers between devices, per_device(): lax.all_gather(gate_weight, 'shard', axis=0, tiled=True)  224 us
    all_gather x1, waiting for transfers between devices, per_device(): lax.all_gather(down_weight, 'shard', axis=0, tiled=True)  216 us
    all_gather x1, waiting for transfers between devices, per_device(): lax.all_gather(up_weight, 'shard', axis=0, tiled=True)  216 us
    all_gather x1, waiting for transfers between devices, per_device(): piece_mlp = lax.all_gather(grad_mlp, 'shard', axis=0, tiled=True)  118 us
    all_gather x1, waiting for transfers between devices, per_device(): lax.all_gather(query_weight, 'shard', axis=0, tiled=True)  87.6 us
    dot_general x7, matrix products, dims_last(): lax.dot_general(left_op, right_op, (((1,), (1,)), ((), ())), preferred_el...  63.7 us
    all_gather x1, waiting for transfers between devices, per_device(): lax.all_gather(out_weight, 'shard', axis=0, tiled=True)  60.5 us
  transfers between devices with their start and end apart: 20, of which 17 were waited for; matrix products, arithmetic and copies ran while one was open for 8% of the time, Pallas kernels for 0%

commit v1 on v0

--- a/solution.py
+++ b/solution.py
@@ -12,6 +12,20 @@
 EPSILON = 1e-06
 ROPE_BASE = 1000000.0
 MASKED = -1e30
+
+
+def trace_face_for(in_array, comm_axis):
+    r1 = lax.axis_index(comm_axis)
+    value_now = lax.axis_size(comm_axis)
+    passed, field_out, outer = (value_now, r1, in_array.shape[0])
+    earlier, current_block = (in_array, 1)
+    while current_block < passed:
+        y_new = lax.ppermute(
+            earlier, comm_axis, [(tick, (tick - current_block) % passed) for tick in range(passed)]
+        )
+        earlier = jnp.concatenate([earlier, y_new], axis=0)
+        current_block = 2 * current_block
+    return jnp.roll(earlier, field_out * outer, axis=0)
 
 
 def dims_last(left_op, right_op):
@@ -189,7 +203,7 @@
     normed_mlp = (hidden * rstat_mlp * mlp_gain).astype(jnp.bfloat16)
     full_gate, full_up, full_down = (
         lax.all_gather(gate_weight, "shard", axis=0, tiled=True),
-        lax.all_gather(up_weight, "shard", axis=0, tiled=True),
+        trace_face_for(up_weight, "shard"),
         lax.all_gather(down_weight, "shard", axis=0, tiled=True),
     )
     gate_pre = jnp.dot(normed_mlp, full_gate, preferred_element_type=jnp.float32)

time: 2090 us -> 2380 us (1.14)
  waiting for transfers between devices: 1630 us -> 1860 us
  local copies, waits for them, and re-layouts: 91.2 us -> 129 us
    ppermute x0 -> x2, waiting for transfers between devices: none -> 234 us  [trace_face_for(): lax.ppermute(earlier, comm_axis, [(tick, (tick - current_block) % passed)...]
    all_gather x1, waiting for transfers between devices: 216 us -> 137 us  [per_device(): lax.all_gather(down_weight, 'shard', axis=0, tiled=True)]
    all_gather x1, waiting for transfers between devices: 60.5 us -> 128 us  [per_device(): lax.all_gather(out_weight, 'shard', axis=0, tiled=True)]
    all_gather x1, waiting for transfers between devices: 87.6 us -> 149 us  [per_device(): lax.all_gather(query_weight, 'shard', axis=0, tiled=True)]
    all_gather x1, waiting for transfers between devices: 216 us -> 183 us  [per_device(): lax.all_gather(up_weight, 'shard', axis=0, tiled=True)]
    unnamed x93 -> x108, local copies, waits for them, and re-layouts: 18.8 us -> 48 us
  transfers between devices with their start and end apart: 20 -> 22, of which waited for: 17 -> 18; matrix products, arithmetic and copies ran while one was open for 8% -> 11% of each run, Pallas kernels for 0% -> 0%
where the time goes in v1:
time: 2380 us; the launch traced here: 2370 us
  waiting for transfers between devices  1860 us (78%)
  matrix products  231 us (10%)
  local copies, waits for them, and re-layouts  129 us (5%)
  other arithmetic  70.5 us (3%)
  blocking collectives  41.9 us (2%)
    psum x1, waiting for transfers between devices, per_device(): lax.psum(added_in.astype(jnp.bfloat16), 'rep').astype(jnp.float32)  424 us
    ppermute x2, waiting for transfers between devices, trace_face_for(): lax.ppermute(earlier, comm_axis, [(tick, (tick - current_block) % passed)...  234 us
    all_gather x1, waiting for transfers between devices, per_device(): lax.all_gather(gate_weight, 'shard', axis=0, tiled=True)  214 us
    all_gather x1, waiting for transfers between devices, per_device(): lax.all_gather(up_weight, 'shard', axis=0, tiled=True)  183 us
    all_gather x1, waiting for transfers between devices, per_device(): lax.all_gather(query_weight, 'shard', axis=0, tiled=True)  149 us
    all_gather x1, waiting for transfers between devices, per_device(): lax.all_gather(down_weight, 'shard', axis=0, tiled=True)  137 us
    all_gather x1, waiting for transfers between devices, per_device(): lax.all_gather(out_weight, 'shard', axis=0, tiled=True)  128 us
    all_gather x1, waiting for transfers between devices, per_device(): piece_mlp = lax.all_gather(grad_mlp, 'shard', axis=0, tiled=True)  118 us
  transfers between devices with their start and end apart: 22, of which 18 were waited for; matrix products, arithmetic and copies ran while one was open for 11% of the time, Pallas kernels for 0%

profile of v1, /device:TPU:0, one launch (start us, length us, event | category | flops | bytes accessed | tf_op | source)
XLA Modules:
  0.0 2370.0 jit_solution(1633411157119126199)
XLA Ops:
  11.7 53.4 %all-gather.19.cloned.1.call-done = bf16[2048,1024]{1,0:T(8,128)(2,1)} async-done(((bf16[512,1024]{1,0:T(8,128)(2,1)}), bf16[2048,1024]{1,0:T(8,128)(2,1)}) %all-gather.19.cloned.1.call-update) | async-done | bytes 4194320 | tf_op jit(solution)/shard_map/all_gather | solution.py:170
  65.2 6.4 copy.79
  71.6 3.7 multiply_reduce_fusion.9
  77.7 41.9 %all-gather.15.cloned.1.call-done = bf16[2048,1024]{1,0:T(8,128)(2,1)} async-done(((bf16[512,1024]{1,0:T(8,128)(2,1)}), bf16[2048,1024]{1,0:T(8,128)(2,1)}) %all-gather.15.cloned.1.call-update) | async-done | bytes 4194320 | tf_op jit(solution)/shard_map/all_gather | solution.py:171
  119.6 3.0 fusion.55
  130.0 136.7 %collective-permute-done = bf16[512,6144]{1,0:T(8,128)(2,1)} collective-permute-done((bf16[512,6144]{1,0:T(8,128)(2,1)}, bf16[512,6144]{1,0:T(8,128)(2,1)}, u32[]{:S(2)}, u32[]{:S(2)}) %collective-permute-start) | collective-permute-done | bytes 6291488 | tf_op jit(solution)/shard_map/ppermute | solution.py:23
  266.7 10.4 pad_maximum_fusion.1
  278.6 3.0 constant_dynamic-update-slice_fusion.7
  281.6 6.2 constant_dynamic-update-slice_fusion.6
  289.5 148.8 %all-gather.23.cloned.1.call-done = bf16[2048,2048]{1,0:T(8,128)(2,1)} async-done(((bf16[512,2048]{1,0:T(8,128)(2,1)}), bf16[2048,2048]{1,0:T(8,128)(2,1)}) %all-gather.23.cloned.1.call-update) | async-done | bytes 8388624 | tf_op jit(solution)/shard_map/all_gather | solution.py:169
  438.3 12.2 copy.80
  450.6 5.8 multiply_reduce_fusion.6
  460.4 15.4 all-gather.17.cloned.1.call-done
  475.7 28.5 %while.30 = (s32[]{:T(128)}, bf16[8,128,2,128]{1,3,2,0:T(8,128)(2,1)}, f32[8,2,128,1]{2,1,3,0:T(2,128)}, bf16[8,512,128]{2,1,0:T(8,128)(2,1)}, bf16[8,512,128]{2...) while((s32[]{:T(128)}, ...), condition=%wide.region_8.9_spmd.clone.clone, body=%wide.region_5.8_spmd.clone.sunk.clone | while | flops 68353792 | bytes 2176605 | solution.py:194
  504.2 128.4 %all-gather.25.cloned.1.call-done = bf16[2048,2048]{1,0:T(8,128)(2,1)} async-done(((bf16[512,2048]{1,0:T(8,128)(2,1)}), bf16[2048,2048]{1,0:T(8,128)(2,1)}) %all-gather.25.cloned.1.call-update) | async-done | bytes 8388624 | tf_op jit(solution)/shard_map/all_gather | solution.py:172
  632.6 4.9 multiply_reduce_fusion.5
  638.5 97.4 %collective-permute-done.1 = bf16[1024,6144]{1,0:T(8,128)(2,1)} collective-permute-done((bf16[1024,6144]{1,0:T(8,128)(2,1)}, bf16[1024,6144]{1,0:T(8,128)(2,1)}, u32[]{:S(2)}, u32[]{:S(2)}) %collective-permute-start.1) | collective-permute-done | bytes 12582944 | tf_op jit(solution)/shard_map/ppermute | solution.py:23
  735.9 10.7 constant_dynamic-update-slice_fusion.5
  746.6 3.1 constant_dynamic-update-slice_fusion.4
  749.7 6.3 constant_dynamic-update-slice_fusion.3
  756.0 10.8 constant_dynamic-update-slice_fusion.2
  766.7 136.9 %all-gather.29.cloned.1.call-done = bf16[6144,2048]{1,0:T(8,128)(2,1)} async-done(((bf16[1536,2048]{1,0:T(8,128)(2,1)}), bf16[6144,2048]{1,0:T(8,128)(2,1)}) %all-gather.29.cloned.1.call-update) | async-done | bytes 25165840 | tf_op jit(solution)/shard_map/all_gather | solution.py:207
  903.6 15.2 fusion.74
  918.9 214.2 %all-gather.27.cloned.1.call-done = bf16[2048,6144]{1,0:T(8,128)(2,1)} async-done(((bf16[512,6144]{1,0:T(8,128)(2,1)}), bf16[2048,6144]{1,0:T(8,128)(2,1)}) %all-gather.27.cloned.1.call-update) | async-done | bytes 25165840 | tf_op jit(solution)/shard_map/all_gather | solution.py:205
  1133.1 13.9 fusion.89
  1147.0 18.0 multiply_convert_fusion.1
  1165.0 14.3 fusion.90
  1179.3 183.3 %all-gather.31.cloned.1.call-done = bf16[2048,6144]{1,0:T(8,128)(2,1)} async-done(((bf16[512,6144]{1,0:T(8,128)(2,1)}), bf16[2048,6144]{1,0:T(8,128)(2,1)}) %all-gather.31.cloned.1.call-update) | async-done | bytes 25165840 | tf_op jit(solution)/shard_map/all_gather | solution.py:218
  1362.6 15.6 multiply_reduce_fusion.1
  1380.6 6.4 convolution_convert_fusion.4
  1390.2 86.7 %while.31 = (s32[]{:T(128)}, f32[8,128,2,128]{1,3,2,0:T(8,128)}, bf16[8,512,128]{1,2,0:T(8,128)(2,1)}, bf16[8,512,128]{1,2,0:T(8,128)(2,1)}, bf16[8,512,128]{2,1...) while((s32[]{:T(128)}, f32[8,128,2,128]{1,3,2,0:T(8,128)}, ...), condition=%wide.region_13.14_spmd.clone.clone, body=%wide.region_11.13_spmd.clone.sunk.clone | while | flops 169312000 | bytes 5780601 | solution.py:238
  1476.9 2.4 copy.97
  1479.3 2.5 copy.138
  1481.9 2.4 copy.99
  1484.3 2.5 copy.137
  1491.1 18.8 reduce-scatter.7.cloned.1.call-done
  1511.2 30.2 %reduce-scatter.9.cloned.1.call-done = bf16[128,1024]{1,0:T(8,128)(2,1)} async-done(((bf16[512,1024]{1,0:T(8,128)(2,1)}), bf16[128,1024]{1,0:T(8,128)(2,1)}) %reduce-scatter.9.cloned.1.call-update) | async-done | bytes 262160
  1544.9 3.8 pad_maximum_fusion.2
  1548.8 3.6 all-to-all-start.2
  1552.4 2.7 copy.136
  1555.1 9.4 all-to-all-done.2
  1564.5 4.4 all-to-all-start.3
  1574.0 25.6 %all-to-all-done.3 = bf16[128,4,1536]{2,0,1:T(8,128)(2,1)} async-done(((bf16[128,4,1536]{2,0,1:T(8,128)(2,1)}), bf16[128,4,1536]{2,0,1:T(8,128)(2,1)}, u32[]{:S(2)}, u32[]{:S(2)}) %all-to-all-start.3) | async-done | bytes 1572896 | tf_op jit(solution)/shard_map/all_to_all | solution.py:279
  1599.6 3.6 all-to-all-start
  1603.3 8.2 convolution_convert_fusion.1
  1611.6 25.3 %all-gather.37.cloned.1.call-done = bf16[512,2048]{1,0:T(8,128)(2,1)} async-done(((bf16[128,2048]{1,0:T(8,128)(2,1)}), bf16[512,2048]{1,0:T(8,128)(2,1)}) %all-gather.37.cloned.1.call-update) | async-done | bytes 2097168 | tf_op jit(solution)/shard_map/all_gather | solution.py:283
  1636.9 4.2 convolution_convert_fusion.3
  1641.0 3.5 all-to-all-start.1
  1644.6 49.5 %all-gather.33.cloned.1.call-done = bf16[512,4096]{0,1:T(8,128)(2,1)} async-done(((bf16[128,4096]{0,1:T(8,128)(2,1)}), bf16[512,4096]{0,1:T(8,128)(2,1)}) %all-gather.33.cloned.1.call-update) | async-done | bytes 4194320 | tf_op jit(solution)/shard_map/all_gather | solution.py:281
  1694.1 6.6 convolution_convert_fusion.2
  1700.7 118.1 %all-gather.35.cloned.1.call-done = bf16[512,12288]{1,0:T(8,128)(2,1)} async-done(((bf16[128,12288]{1,0:T(8,128)(2,1)}), bf16[512,12288]{1,0:T(8,128)(2,1)}) %all-gather.35.cloned.1.call-update) | async-done | bytes 12582928 | tf_op jit(solution)/shard_map/all_gather | solution.py:282
  1818.8 11.7 convolution_convert_fusion
  1830.5 8.9 pad_maximum_fusion
  1839.5 6.4 fusion.91
  1845.9 11.3 fusion.53
  1859.5 2.7 fusion.69
  1862.1 41.9 %all-reduce = (f32[2048]{0:T(1024)}, f32[128]{0:T(128)}, f32[128]{0:T(128)}, f32[2048]{0:T(1024)}) all-reduce(f32[2048]{0:T(1024)S(1)} %get-tuple-element.250, f32[128]{0:T(128)S(1)} %get-tuple-element.246, f32[128]{0:T(128)S(1)} %get-tuple-element.252, f32[2048]{0:T(1024)S(1)} %copy-done.30), channel_id=1, replica_groups=mesh['shard'=4,'rep'=8] {'shard','rep'}, use_global_device_ids=true, to_apply=%region_20.21 | all-reduce | flops 4352 | bytes 34816 | tf_op jit(solution)/shard_map/psum | solution.py:270
  1904.1 2.8 fusion.68
  1906.9 424.3 %all-reduce.4.cloned.1.call-done = (bf16[512,16384]{1,0:T(8,128)(2,1)}, bf16[512,2048]{1,0:T(8,128)(2,1)}, bf16[1536,2048]{1,0:T(8,128)(2,1)}) async-done(((bf16[512,16384]{1,0:T(8,128)(2,1)}, bf16[512,2048]{1,0:T(8,128)(2,1)}, bf16[1536,2048]{1,0:T(8,128)(2,1)}), (bf16[512,16384]{1,0:T(8,128)(2,1)}, bf16[512,2048]{1,0:T(8,128)(2,1)}, bf16[1536,2048]{1,0:T(8,128)(2,1)})) %all-reduce.4.cloned.1.call-update) | async-done | bytes 25165840 | tf_op jit(solution)/shard_map/psum | solution.py:291
  2331.2 15.6 fusion.87
  2349.2 2.6 fusion.88
  2351.8 2.5 slice.77
  2354.4 6.3 convert_element_type.162
  2360.7 2.5 convert_element_type.160
  (312 shorter events, 161.3 us)
Async XLA Ops:
  7.2 64.4 %copy-start.1 = (bf16[1,128,2048]{2,1,0:T(8,128)(2,1)S(1)}, bf16[1,128,2048]{2,1,0:T(8,128)(2,1)}, u32[]{:S(2)}) copy-start(bf16[1,128,2048]{2,1,0:T(8,128)(2,1)} %param.18) | copy-start | bytes 1572868
  7.2 64.4 %copy-start.25 = (f32[2048]{0:T(1024)S(1)}, f32[2048]{0:T(1024)}, u32[]{:S(2)}) copy-start(f32[2048]{0:T(1024)} %param.20) | copy-start | bytes 24580
  7.2 58.0 %all-gather.19.cloned.1.call-start = ((), (), s32[]{:S(2)}) async-start(), calls=%async_computation.8 | async-start | bytes 5242880 | tf_op jit(solution)/shard_map/all_gather | solution.py:170
  7.9 111.7 %all-gather.15.cloned.1.call-start = ((), (), s32[]{:S(2)}) async-start(), calls=%async_computation.6 | async-start | bytes 5242880 | tf_op jit(solution)/shard_map/all_gather | solution.py:171
  8.7 279.2 %all-gather.21.cloned.1.call-start = ((), (), s32[]{:S(2)}) async-start(), calls=%async_computation.9 | async-start | bytes 1310720 | tf_op jit(solution)/shard_map/all_gather | solution.py:190
  11.5 439.0 %copy-start.31 = (f32[128]{0:T(128)}, f32[128]{0:T(128)S(1)}, u32[]{:S(2)}) copy-start(f32[128]{0:T(128)S(1)} %add_rsqrt_fusion.3) | copy-start | bytes 1540
  11.7 444.9 %copy-start.20 = (f32[128,64]{0,1:T(8,128)}, f32[128,64]{0,1:T(8,128)S(1)}, u32[]{:S(2)}) copy-start(f32[128,64]{0,1:T(8,128)S(1)} %get-tuple-element.322) | copy-start | bytes 98308
  11.7 444.9 %copy-start.22 = (f32[128,64]{0,1:T(8,128)}, f32[128,64]{0,1:T(8,128)S(1)}, u32[]{:S(2)}) copy-start(f32[128,64]{0,1:T(8,128)S(1)} %get-tuple-element.323) | copy-start | bytes 98308
  65.2 11.0 copy-start.35
  77.1 361.2 %all-gather.23.cloned.1.call-start = ((), (), s32[]{:S(2)}) async-start(), calls=%async_computation.10 | async-start | bytes 10485760 | tf_op jit(solution)/shard_map/all_gather | solution.py:169
  77.7 398.1 %all-gather.17.cloned.1.call-start = ((), (), s32[]{:S(2)}) async-start(), calls=%async_computation.7 | async-start | bytes 1310720 | tf_op jit(solution)/shard_map/all_gather | solution.py:191
  123.4 509.2 %all-gather.25.cloned.1.call-start = ((), (), s32[]{:S(2)}) async-start(), calls=%async_computation.11 | async-start | bytes 10485760 | tf_op jit(solution)/shard_map/all_gather | solution.py:172
  123.9 779.7 %all-gather.29.cloned.1.call-start = ((), (), s32[]{:S(2)}) async-start(), calls=%async_computation.13 | async-start | bytes 31457280 | tf_op jit(solution)/shard_map/all_gather | solution.py:207
  124.7 3.2 copy-start.24
  124.7 1008.4 %all-gather.27.cloned.1.call-start = ((), (), s32[]{:S(2)}) async-start(), calls=%async_computation.12 | async-start | bytes 31457280 | tf_op jit(solution)/shard_map/all_gather | solution.py:205
  125.5 1237.1 %all-gather.31.cloned.1.call-start = ((), (), s32[]{:S(2)}) async-start(), calls=%async_computation.14 | async-start | bytes 31457280 | tf_op jit(solution)/shard_map/all_gather | solution.py:218
  126.2 1383.8 %reduce-scatter.7.cloned.1.call-start = ((), (), s32[]{:S(2)}) async-start(), calls=%async_computation.19 | async-start | bytes 1310720
  126.2 140.4 %collective-permute-start = (bf16[512,6144]{1,0:T(8,128)(2,1)}, bf16[512,6144]{1,0:T(8,128)(2,1)}, u32[]{:S(2)}, u32[]{:S(2)}) collective-permute-start(bf16[512,6144]{1,0:T(8,128)(2,1)} %param.29), channel_id=1, source_target_pairs={{0,24},{8,0},{16,8},{24,16},{1,25},{9,1},{17,9},{25,17},{2,26},{10... | collective-permute-start | bytes 18874376 | tf_op jit(solution)/shard_map/ppermute | solution.py:23
  129.1 149.5 %slice-start = ((s8[6291456]{0:T(1024)(128)(4,1)}), s8[4194304]{0:T(1024)(128)(4,1)S(1)}, s32[]{:S(2)}) async-start(s8[6291456]{0:T(1024)(128)(4,1)} %bitcast.322), calls=%async_computation.22 | async-start | bytes 8388608
  130.0 148.6 %slice-start.1 = ((s8[6291456]{0:T(1024)(128)(4,1)}), s8[2097152]{0:T(1024)(128)(4,1)S(1)}, s32[]{:S(2)}) async-start(s8[6291456]{0:T(1024)(128)(4,1)} %bitcast.322), calls=%async_computation.23 | async-start | bytes 4194304
  277.1 458.7 %collective-permute-start.1 = (bf16[1024,6144]{1,0:T(8,128)(2,1)}, bf16[1024,6144]{1,0:T(8,128)(2,1)}, u32[]{:S(2)}, u32[]{:S(2)}) collective-permute-start(bf16[1024,6144]{1,0:T(8,128)(2,1)} %pad_maximum_fusion.1), channel_id=1, source_target_pairs={{0,16},{8,24},{16,0},{24,8},{1,17},{9,25},{17,1},{25,9},{2,18},{10... | collective-permute-start | bytes 37748744 | tf_op jit(solution)/shard_map/ppermute | solution.py:23
  450.6 5.9 copy-start.37
  456.4 19.3 copy-start.28
  504.2 128.4 %copy-start.7 = (bf16[8,512,128]{2,1,0:T(8,128)(2,1)}, bf16[8,512,128]{2,1,0:T(8,128)(2,1)S(1)}, u32[]{:S(2)}) copy-start(bf16[8,512,128]{2,1,0:T(8,128)(2,1)S(1)} %get-tuple-element.621) | copy-start | bytes 3145732
  504.2 128.4 %copy-start.14 = (bf16[8,128,2,128]{3,1,2,0:T(8,128)(2,1)}, bf16[8,128,2,128]{3,1,2,0:T(8,128)(2,1)S(1)}, u32[]{:S(2)}) copy-start(bf16[8,128,2,128]{3,1,2,0:T(8,128)(2,1)S(1)} %get-tuple-element.633) | copy-start | bytes 1572868
  632.6 5.0 copy-start.26
  637.5 740.7 %copy-start.33 = (f32[128]{0:T(128)}, f32[128]{0:T(128)S(1)}, u32[]{:S(2)}) copy-start(f32[128]{0:T(128)S(1)} %add_rsqrt_fusion.2) | copy-start | bytes 1540
  637.5 109.1 %slice-start.2 = ((s8[6291456]{0:T(1024)(128)(4,1)}), s8[4194304]{0:T(1024)(128)(4,1)S(1)}, s32[]{:S(2)}) async-start(s8[6291456]{0:T(1024)(128)(4,1)} %bitcast.324), calls=%async_computation.24 | async-start | bytes 8388608
  638.5 108.1 %slice-start.3 = ((s8[6291456]{0:T(1024)(128)(4,1)}), s8[2097152]{0:T(1024)(128)(4,1)S(1)}, s32[]{:S(2)}) async-start(s8[6291456]{0:T(1024)(128)(4,1)} %bitcast.324), calls=%async_computation.25 | async-start | bytes 4194304
  756.0 147.7 %copy-start.4 = (bf16[1,128,2048]{2,1,0:T(8,128)(2,1)S(1)}, bf16[1,128,2048]{2,1,0:T(8,128)(2,1)}, u32[]{:S(2)}) copy-start(bf16[1,128,2048]{2,1,0:T(8,128)(2,1)} %param.31) | copy-start | bytes 1572868
  1133.1 13.9 copy-start.11
  1378.2 8.8 copy-start.39
  1476.9 11.3 copy-start.21
  1476.9 11.3 copy-start.23
  1479.3 10.3 copy-start.29
  1479.3 10.3 copy-start.38
  1481.9 59.5 %reduce-scatter.9.cloned.1.call-start = ((), (), s32[]{:S(2)}) async-start(), calls=%async_computation.20 | async-start | bytes 1310720
  1486.8 55.9 %copy-start.9 = (f32[128,8,128]{0,2,1:T(8,128)S(1)}, f32[128,8,128]{0,2,1:T(8,128)}, u32[]{:S(2)}) copy-start(f32[128,8,128]{0,2,1:T(8,128)} %copy-done.8) | copy-start | bytes 1572868
  1486.8 55.9 %copy-start.36 = (f32[128]{0:T(128)S(1)}, f32[128]{0:T(128)}, u32[]{:S(2)}) copy-start(f32[128]{0:T(128)} %param.25) | copy-start | bytes 1540
  1486.8 116.5 %all-gather.39.cloned.1.call-start = ((), (), s32[]{:S(2)}) async-start(), calls=%async_computation.18 | async-start | bytes 2621440 | tf_op jit(solution)/shard_map/all_gather | solution.py:284
  1487.4 149.4 %all-gather.37.cloned.1.call-start = ((), (), s32[]{:S(2)}) async-start(), calls=%async_computation.17 | async-start | bytes 2621440 | tf_op jit(solution)/shard_map/all_gather | solution.py:283
  1488.2 205.9 %all-gather.33.cloned.1.call-start = ((), (), s32[]{:S(2)}) async-start(), calls=%async_computation.15 | async-start | bytes 5242880 | tf_op jit(solution)/shard_map/all_gather | solution.py:281
  1491.1 52.6 %copy-start.13 = (bf16[128,16,128]{0,2,1:T(8,128)(2,1)S(1)}, bf16[128,16,128]{0,2,1:T(8,128)(2,1)}, u32[]{:S(2)}) copy-start(bf16[128,16,128]{0,2,1:T(8,128)(2,1)} %multiply_convert_fusion.4) | copy-start | bytes 1572868
  1542.6 6.1 copy-start.17
  1544.9 273.9 %all-gather.35.cloned.1.call-start = ((), (), s32[]{:S(2)}) async-start(), calls=%async_computation.16 | async-start | bytes 15728640 | tf_op jit(solution)/shard_map/all_gather | solution.py:282
  1548.7 21.9 copy-start.32
  1548.7 24.3 %copy-start.12 = (bf16[128,2048]{1,0:T(8,128)(2,1)S(1)}, bf16[128,2048]{1,0:T(8,128)(2,1)}, u32[]{:S(2)}) copy-start(bf16[128,2048]{1,0:T(8,128)(2,1)} %multiply_convert_fusion.5) | copy-start | bytes 1572868
  1548.8 15.8 all-to-all-start.2
  1564.5 35.1 %all-to-all-start.3 = ((bf16[128,4,1536]{2,0,1:T(8,128)(2,1)}), bf16[128,4,1536]{2,0,1:T(8,128)(2,1)}, u32[]{:S(2)}, u32[]{:S(2)}) async-start(bf16[128,4,1536]{2,0,1:T(8,128)(2,1)} %bitcast.331), calls=%async_computation.3 | async-start | bytes 3145728 | tf_op jit(solution)/shard_map/all_to_all | solution.py:279
  1599.6 41.4 %all-to-all-start = ((bf16[128,4,512]{2,0,1:T(8,128)(2,1)}), bf16[128,4,512]{2,0,1:T(8,128)(2,1)S(1)}, u32[]{:S(2)}, u32[]{:S(2)}) async-start(bf16[128,4,512]{2,0,1:T(8,128)(2,1)} %fusion.58), calls=%async_computation | async-start | bytes 1048576 | tf_op jit(solution)/shard_map/all_to_all | solution.py:276
  1641.0 59.7 %all-to-all-start.1 = ((bf16[128,4,512]{2,0,1:T(8,128)(2,1)}), bf16[128,4,512]{2,0,1:T(8,128)(2,1)S(1)}, u32[]{:S(2)}, u32[]{:S(2)}) async-start(bf16[128,4,512]{2,0,1:T(8,128)(2,1)} %bitcast.257), calls=%async_computation.1 | async-start | bytes 1048576 | tf_op jit(solution)/shard_map/all_to_all | solution.py:277
  1644.5 686.7 %all-reduce.4.cloned.1.call-start = ((), (), s32[]{:S(2)}) async-start(), calls=%async_computation.21 | async-start | bytes 50331648 | tf_op jit(solution)/shard_map/psum | solution.py:291
  1839.5 6.4 copy-start.10
  1845.9 11.3 copy-start.3
  1845.9 11.3 copy-start.16
  1857.2 4.9 copy-start.30
  1857.2 46.8 %copy-start.5 = (bf16[1,128,2048]{2,1,0:T(8,128)(2,1)S(1)}, bf16[1,128,2048]{2,1,0:T(8,128)(2,1)}, u32[]{:S(2)}) copy-start(bf16[1,128,2048]{2,1,0:T(8,128)(2,1)} %param.31) | copy-start | bytes 1572868
  1857.2 46.8 %copy-start.6 = (f32[128,2048]{1,0:T(8,128)S(1)}, f32[128,2048]{1,0:T(8,128)}, u32[]{:S(2)}) copy-start(f32[128,2048]{1,0:T(8,128)} %get-tuple-element.330) | copy-start | bytes 3145732
  1857.2 46.8 %copy-start.27 = (f32[2048]{0:T(1024)S(1)}, f32[2048]{0:T(1024)}, u32[]{:S(2)}) copy-start(f32[2048]{0:T(1024)} %param.27) | copy-start | bytes 24580
  1857.3 46.8 %copy-start.34 = (f32[128]{0:T(128)S(1)}, f32[128]{0:T(128)}, u32[]{:S(2)}) copy-start(f32[128]{0:T(128)} %copy-done.33) | copy-start | bytes 1540
  1857.3 46.8 %copy-start.40 = (f32[128]{0:T(128)S(1)}, f32[128]{0:T(128)}, u32[]{:S(2)}) copy-start(f32[128]{0:T(128)} %copy-done.39) | copy-start | bytes 1540
  2331.2 18.0 copy-start
  2349.2 5.1 slice-start.4
  2354.4 6.3 copy-start.19
  (5 other events, 8.6 us)
Sparse Core Ops, SparseCore 0:
  9.9 55.2 all-gather.18
  67.0 52.5 all-gather.14
  122.0 160.2 all-gather.20
  284.0 154.2 all-gather.22
  440.6 35.1 all-gather.16
  477.4 155.0 all-gather.24
  634.4 269.1 all-gather.28
  905.5 227.5 all-gather.26
  1135.0 227.5 all-gather.30
  1482.0 27.9 reduce-scatter.6
  1513.4 27.9 reduce-scatter.8
  1543.1 56.6 all-gather.38
  1601.7 35.1 all-gather.36
  1639.1 54.9 all-gather.32
  1696.4 122.3 all-gather.34
  1839.6 491.5 all-reduce.3
